TPU v7x, 768 devices: a whole 4x8x12 slice. The times are simulated.
768 devices in a mesh: seq: 96 (over z, x, core), head: 8 (over y).
Axes of the slice: x: 4, y: 8, z: 12, core: 2. Of those that a mesh axis runs over, the one named last changes fastest.
Arguments:
- queries: bfloat16 [49152, 4096], P('seq', 'head'), may hold values from -360 to 360, as said below
- key_rows: bfloat16 [49152, 1024], P('seq', 'head'), may hold values from -6 to 6
- value_rows: bfloat16 [49152, 1024], P('seq', 'head'), may hold values from -6 to 6
- doc_lengths: int32 [96], replicated, may hold values from 1 to 1536, 49152 in all
Outputs:
- attn_out: bfloat16 [49152, 4096], P(('seq', 'head'))
Inputs may be any that keep to these rules, and one draw needn't show every extreme that they name: `queries`: custom draw of bounded query entries. `doc_lengths`: the lengths sum to 49152; each is at most 1536.
All inputs are finite; a program needn't handle non-finite values.
Results may differ from a plain program's by a relative error of at most 0.0036.
Values may be sent and summed in bfloat16 or wider, within the bound.
No kernel may reach another device: no remote copies, remote signals or barrier semaphores. Data moves between devices by JAX's collectives and lax.ppermute only.
A program may use at most 32 MiB of HBM per device.

v0:
```python
import jax
import jax.numpy as jnp
from jax import lax
from jax.sharding import PartitionSpec as P

H = 32
KVH = 8
HD = 128
SPAN = 4


scaling = 0.08838834764831845


def from_behind(x, axis, by):
    peers = lax.axis_size(axis)
    pairs = [(i, i + by) for i in range(peers) if 0 <= i + by < peers]
    return lax.ppermute(x, axis, pairs)


def doc_index(ends, positions):
    return jnp.sum((ends[None, :] <= positions[:, None]).astype(jnp.int32), axis=1)


def per_device(queries, key_rows, value_rows, doc_lengths):
    tokens_here = queries.shape[0]
    group = H // KVH
    key_window = key_rows
    value_window = value_rows
    for level in range(SPAN.bit_length() - 1):
        moved = from_behind((key_window, value_window), "seq", 1 << level)
        key_window = jnp.concatenate([moved[0], key_window], 0)
        value_window = jnp.concatenate([moved[1], value_window], 0)
    ends = jnp.cumsum(doc_lengths)
    first = lax.axis_index("seq") * tokens_here
    query_pos = first + jnp.arange(tokens_here, dtype=jnp.int32)
    key_pos = first - (SPAN - 1) * tokens_here + jnp.arange(SPAN * tokens_here, dtype=jnp.int32)
    allowed = (
        (key_pos[None, :] >= 0)
        & (doc_index(ends, key_pos)[None, :] == doc_index(ends, query_pos)[:, None])
        & (key_pos[None, :] <= query_pos[:, None])
    )
    outputs = []
    for member in range(group):
        column = member * HD
        query_head = queries[:, column : column + HD]
        scores = (
            lax.dot_general(
                query_head, key_window, (((1,), (1,)), ((), ())), preferred_element_type=jnp.float32
            )
            * scaling
        )
        scores = jnp.where(allowed, scores, jnp.float32(-1e30))
        largest = jnp.max(scores, axis=1, keepdims=True)
        weights = jnp.where(allowed, jnp.exp(scores - largest), jnp.float32(0.0))
        total = jnp.sum(weights, axis=1, keepdims=True)
        mixed = jnp.dot(
            weights.astype(jnp.bfloat16), value_window, preferred_element_type=jnp.float32
        )
        outputs.append((mixed / total).astype(jnp.bfloat16))
    merged = jnp.concatenate(outputs, 1)
    return lax.all_to_all(merged, "head", split_axis=0, concat_axis=1, tiled=True)


def solution(mesh):
    in_specs = (P("seq", "head"), P("seq", "head"), P("seq", "head"), P())
    out_specs = P(("seq", "head"), None)
    return jax.shard_map(
        per_device, mesh=mesh, in_specs=in_specs, out_specs=out_specs, check_vma=False
    )
```

profile of v0, /device:TPU:512, one launch (start us, length us, event | category | flops | bytes accessed | tf_op | source)
XLA Modules:
  0.0 70.0 jit_solution(11010563661597637589)
XLA Ops:
  0.0 0.0 copy-start.1
  0.0 2.0 %collective-permute-start = (bf16[512,128]{1,0:T(8,128)(2,1)}, bf16[512,128]{1,0:T(8,128)(2,1)S(1)}, u32[]{:S(2)}, u32[]{:S(2)}) collective-permute-start(bf16[512,128]{1,0:T(8,128)(2,1)} %param.5), channel_id=1, source_target_pairs={{0,8},{8,16},{16,24},{24,32},{32,40},{40,48},{48,56},{56,64},{64,7... | collective-permute-start | bytes 393224 | tf_op jit(solution)/shard_map/ppermute | solution.py:18
  2.1 3.5 %collective-permute-start.2 = (bf16[512,128]{1,0:T(8,128)(2,1)}, bf16[512,128]{1,0:T(8,128)(2,1)S(1)}, u32[]{:S(2)}, u32[]{:S(2)}) collective-permute-start(bf16[512,128]{1,0:T(8,128)(2,1)} %param.6), channel_id=1, source_target_pairs={{0,8},{8,16},{16,24},{24,32},{32,40},{40,48},{48,56},{56,64},{64,7... | collective-permute-start | bytes 393224 | tf_op jit(solution)/shard_map/ppermute | solution.py:18
  5.6 0.8 %copy.12 = s32[96,1]{1,0:T(8,128)S(1)} copy(s32[96,1]{0,1:T(1,128)} %bitcast.75) | data formatting | bytes 768 | tf_op jit(solution)/shard_map/reshape.45
  6.4 0.1 reduce-window.8
  6.5 0.1 reduce
  6.6 0.1 convert_reduce_fusion.1
  6.7 3.2 %collective-permute-done = bf16[512,128]{1,0:T(8,128)(2,1)S(1)} collective-permute-done((bf16[512,128]{1,0:T(8,128)(2,1)}, bf16[512,128]{1,0:T(8,128)(2,1)S(1)}, u32[]{:S(2)}, u32[]{:S(2)}) %collective-permute-start) | collective-permute-done | bytes 131104 | tf_op jit(solution)/shard_map/ppermute | solution.py:18
  9.9 0.9 %pad_maximum_fusion.1 = bf16[1024,128]{1,0:T(8,128)(2,1)S(1)} fusion(bf16[512,128]{1,0:T(8,128)(2,1)} %param.5, bf16[512,128]{1,0:T(8,128)(2,1)S(1)} %collective-permute-done), kind=kLoop, calls=%fused_computation.35 | loop fusion | flops 524288 | bytes 524288 | tf_op jit(solution)/shard_map/concatenate | solution.py:32
  10.9 1.9 %collective-permute-start.1 = (bf16[1024,128]{1,0:T(8,128)(2,1)S(1)}, bf16[1024,128]{1,0:T(8,128)(2,1)S(1)}, u32[]{:S(2)}, u32[]{:S(2)}) collective-permute-start(bf16[1024,128]{1,0:T(8,128)(2,1)S(1)} %pad_maximum_fusion.1), channel_id=1, source_target_pairs={{0,16},{8,24},{16,32},{24,40},{32,48},{40,56},{48,64},{56,72},{64,... | collective-permute-start | bytes 786440 | tf_op jit(solution)/shard_map/ppermute | solution.py:18
  12.8 0.2 convert_reduce_fusion
  13.0 0.0 collective-permute-done.2
  13.0 0.9 %pad_maximum_fusion.2 = bf16[1024,128]{1,0:T(8,128)(2,1)S(1)} fusion(bf16[512,128]{1,0:T(8,128)(2,1)} %param.6, bf16[512,128]{1,0:T(8,128)(2,1)S(1)} %collective-permute-done.2), kind=kLoop, calls=%fused_computation.36 | loop fusion | flops 524288 | bytes 524288 | tf_op jit(solution)/shard_map/concatenate | solution.py:33
  13.9 1.9 %collective-permute-start.3 = (bf16[1024,128]{1,0:T(8,128)(2,1)S(1)}, bf16[1024,128]{1,0:T(8,128)(2,1)S(1)}, u32[]{:S(2)}, u32[]{:S(2)}) collective-permute-start(bf16[1024,128]{1,0:T(8,128)(2,1)S(1)} %pad_maximum_fusion.2), channel_id=1, source_target_pairs={{0,16},{8,24},{16,32},{24,40},{32,48},{40,56},{48,64},{56,72},{64,... | collective-permute-start | bytes 786440 | tf_op jit(solution)/shard_map/ppermute | solution.py:18
  15.8 9.3 %collective-permute-done.1 = bf16[1024,128]{1,0:T(8,128)(2,1)S(1)} collective-permute-done((bf16[1024,128]{1,0:T(8,128)(2,1)S(1)}, bf16[1024,128]{1,0:T(8,128)(2,1)S(1)}, u32[]{:S(2)}, u32[]{:S(2)}) %collective-permute-start.1) | collective-permute-done | bytes 262176 | tf_op jit(solution)/shard_map/ppermute | solution.py:18
  25.2 0.9 %constant_dynamic-update-slice_fusion = bf16[2048,128]{1,0:T(8,128)(2,1)S(1)} fusion(bf16[2048,128]{1,0:T(8,128)(2,1)S(1)} %constant_dynamic-update-slice_fusion.1, bf16[512,128]{1,0:T(8,128)(2,1)} %param.5), kind=kLoop, calls=%fused_computation.46 | loop fusion | bytes 262144 | tf_op jit(solution)/shard_map/concatenate | solution.py:32
  26.2 0.0 copy-start
  26.2 1.6 %fusion.44 = f32[2048,512]{1,0:T(8,128)S(1)} fusion(bf16[2048,128]{1,0:T(8,128)(2,1)S(1)} %constant_dynamic-update-slice_fusion, bf16[512,512]{1,0:T(8,128)(2,1)} %param.4), kind=kOutput, calls=%fused_computation.38 | convolution fusion | flops 268435456 | bytes 4849664 | tf_op jit(solution)/shard_map/dot_general | solution.py:48
  27.8 0.0 copy-done.1
  27.8 0.7 %fusion.46 = f32[2048,512]{1,0:T(8,128)S(1)} fusion(bf16[2048,128]{1,0:T(8,128)(2,1)S(1)} %constant_dynamic-update-slice_fusion, bf16[512,512]{1,0:T(8,128)(2,1)S(1)} %copy-done.1), kind=kOutput, calls=%fused_computation.40 | convolution fusion | flops 268435456 | bytes 4849664 | tf_op jit(solution)/shard_map/dot_general | solution.py:48
  28.6 0.0 collective-permute-done.3
  28.6 0.0 copy-done
  28.7 1.5 %fusion = (f32[512]{0:T(512)S(1)}, f32[2048,512]{1,0:T(8,128)S(1)}) fusion(s32[512]{0:T(512)S(1)} %iota_add_fusion.1, s32[2048]{0:T(1024)S(1)} %iota_add_fusion, s32[512]{0:T(512)S(1)} %convert_reduce_fusion.1, s32[2048]{0:T(1024)S(1)} %convert_reduce_fusion, pred[2048]{0:T(1024)(128)(4,1)S(1)} %broadcast_compare_fusion, ...), kind=kOutput, calls=%fused_computation.9 | convolution fusion | flops 275774976 | bytes 4874240 | tf_op jit(solution)/shard_map/dot_general | solution.py:48
  30.2 3.5 %fusion.4 = (f32[512]{0:T(512)S(1)}, f32[512]{0:T(512)S(1)}, f32[512]{0:T(512)S(1)}, f32[512]{0:T(512)S(1)}, f32[2048,512]{1,0:T(8,128)S(1)}) fusion(f32[2048,512]{1,0:T(8,128)S(1)} %get-tuple-element.13, f32[512]{0:T(512)S(1)} %get-tuple-element.12, s32[512]{0:T(512)S(1)} %iota_add_fusion.1, s32[2048]{0:T(1024)S(1)} %iota_add_fusion, ...), kind=kOutput, calls=%fused_computation.13 | convolution fusion | flops 287307776 | bytes 17465344 | tf_op jit(solution)/shard_map/dot_general | solution.py:48
  33.7 2.2 %fusion.23 = bf16[512,128]{0,1:T(8,128)(2,1)S(1)} fusion(bf16[2048,128]{1,0:T(8,128)(2,1)S(1)} %constant_dynamic-update-slice_fusion.3, f32[2048,512]{1,0:T(8,128)S(1)} %get-tuple-element.13, f32[512]{0:T(512)S(1)} %get-tuple-element.12, f32[512]{0:T(512)S(1)} %get-tuple-element.5, s32[512]{0:T(512)S(1)} %iota_add_fusion.1, ...), kind=kOutput, calls=%fused_computation.26 | convolution fusion | flops 278003712 | bytes 4876288 | tf_op jit(solution)/shard_map/dot_general | solution.py:57
  35.9 5.0 %fusion.6 = (f32[512]{0:T(512)S(1)}, f32[512]{0:T(512)S(1)}, f32[512]{0:T(512)S(1)}) fusion(f32[2048,512]{1,0:T(8,128)S(1)} %get-tuple-element.14, f32[512]{0:T(512)S(1)} %get-tuple-element.6, s32[512]{0:T(512)S(1)} %iota_add_fusion.1, s32[2048]{0:T(1024)S(1)} %iota_add_fusion, s32[512]{0:T(512)S(1)} %convert_reduce_fusion.1, ...), kind=kLoop, calls=%fused_computation.15 | loop fusion | flops 19921408 | bytes 12617728 | tf_op jit(solution)/shard_map/reduce_sum | solution.py:56
  40.9 2.2 %fusion.41 = bf16[512,128]{0,1:T(8,128)(2,1)S(1)} fusion(bf16[2048,128]{1,0:T(8,128)(2,1)S(1)} %constant_dynamic-update-slice_fusion.3, f32[2048,512]{1,0:T(8,128)S(1)} %fusion.44, f32[512]{0:T(512)S(1)} %get-tuple-element.8, f32[512]{0:T(512)S(1)} %get-tuple-element.11, s32[512]{0:T(512)S(1)} %iota_add_fusion.1, s32[512]{0:T(512)S(1)} %convert_reduce_fusion.1, ...), kind=kOutput, calls=%fused_computation.32 | convolution fusion | flops 278003712 | bytes 4876288 | tf_op jit(solution)/shard_map/dot_general | solution.py:57
  43.1 2.2 %fusion.35 = bf16[512,128]{0,1:T(8,128)(2,1)S(1)} fusion(bf16[2048,128]{1,0:T(8,128)(2,1)S(1)} %constant_dynamic-update-slice_fusion.3, f32[2048,512]{1,0:T(8,128)S(1)} %fusion.46, f32[512]{0:T(512)S(1)} %get-tuple-element.7, f32[512]{0:T(512)S(1)} %get-tuple-element.10, s32[512]{0:T(512)S(1)} %iota_add_fusion.1, s32[512]{0:T(512)S(1)} %convert_reduce_fusion.1, ...), kind=kOutput, calls=%fused_computation.30 | convolution fusion | flops 278003712 | bytes 4876288 | tf_op jit(solution)/shard_map/dot_general | solution.py:57
  45.3 2.2 %fusion.29 = bf16[512,128]{0,1:T(8,128)(2,1)S(1)} fusion(bf16[2048,128]{1,0:T(8,128)(2,1)S(1)} %constant_dynamic-update-slice_fusion.3, f32[2048,512]{1,0:T(8,128)S(1)} %get-tuple-element.14, f32[512]{0:T(512)S(1)} %get-tuple-element.6, f32[512]{0:T(512)S(1)} %get-tuple-element.9, s32[512]{0:T(512)S(1)} %iota_add_fusion.1, ...), kind=kOutput, calls=%fused_computation.28 | convolution fusion | flops 278003712 | bytes 4876288 | tf_op jit(solution)/shard_map/dot_general | solution.py:57
  47.5 0.2 copy.13
  47.7 21.4 %all_to_all.19 = bf16[8,64,512]{2,1,0:T(8,128)(2,1)S(1)} all-to-all(bf16[8,64,512]{2,1,0:T(8,128)(2,1)S(1)} %bitcast.73), channel_id=1, replica_groups=mesh['seq'=96,'head'=8] {'head'}, dimensions={0} | all-to-all | bytes 1048576 | tf_op jit(solution)/shard_map/all_to_all | solution.py:62
  69.2 0.8 %copy.15 = bf16[8,8,8,512]{3,2,0,1:T(8,128)(2,1)} copy(bf16[8,8,8,512]{3,2,1,0:T(8,128)(2,1)S(1)} %bitcast.74) | data formatting | bytes 1048576 | tf_op jit(solution)/shard_map/all_to_all | solution.py:62
  (9 shorter events, 0.2 us)
Async XLA Ops:
  0.0 27.8 %copy-start.1 = (bf16[512,512]{1,0:T(8,128)(2,1)S(1)}, bf16[512,512]{1,0:T(8,128)(2,1)}, u32[]{:S(2)}) copy-start(bf16[512,512]{1,0:T(8,128)(2,1)} %param.4) | copy-start | bytes 1572868
  0.0 9.9 %collective-permute-start = (bf16[512,128]{1,0:T(8,128)(2,1)}, bf16[512,128]{1,0:T(8,128)(2,1)S(1)}, u32[]{:S(2)}, u32[]{:S(2)}) collective-permute-start(bf16[512,128]{1,0:T(8,128)(2,1)} %param.5), channel_id=1, source_target_pairs={{0,8},{8,16},{16,24},{24,32},{32,40},{40,48},{48,56},{56,64},{64,7... | collective-permute-start | bytes 393224 | tf_op jit(solution)/shard_map/ppermute | solution.py:18
  2.1 10.9 %collective-permute-start.2 = (bf16[512,128]{1,0:T(8,128)(2,1)}, bf16[512,128]{1,0:T(8,128)(2,1)S(1)}, u32[]{:S(2)}, u32[]{:S(2)}) collective-permute-start(bf16[512,128]{1,0:T(8,128)(2,1)} %param.6), channel_id=1, source_target_pairs={{0,8},{8,16},{16,24},{24,32},{32,40},{40,48},{48,56},{56,64},{64,7... | collective-permute-start | bytes 393224 | tf_op jit(solution)/shard_map/ppermute | solution.py:18
  10.9 14.3 %collective-permute-start.1 = (bf16[1024,128]{1,0:T(8,128)(2,1)S(1)}, bf16[1024,128]{1,0:T(8,128)(2,1)S(1)}, u32[]{:S(2)}, u32[]{:S(2)}) collective-permute-start(bf16[1024,128]{1,0:T(8,128)(2,1)S(1)} %pad_maximum_fusion.1), channel_id=1, source_target_pairs={{0,16},{8,24},{16,32},{24,40},{32,48},{40,56},{48,64},{56,72},{64,... | collective-permute-start | bytes 786440 | tf_op jit(solution)/shard_map/ppermute | solution.py:18
  13.9 14.6 %collective-permute-start.3 = (bf16[1024,128]{1,0:T(8,128)(2,1)S(1)}, bf16[1024,128]{1,0:T(8,128)(2,1)S(1)}, u32[]{:S(2)}, u32[]{:S(2)}) collective-permute-start(bf16[1024,128]{1,0:T(8,128)(2,1)S(1)} %pad_maximum_fusion.2), channel_id=1, source_target_pairs={{0,16},{8,24},{16,32},{24,40},{32,48},{40,56},{48,64},{56,72},{64,... | collective-permute-start | bytes 786440 | tf_op jit(solution)/shard_map/ppermute | solution.py:18
  26.2 2.5 %copy-start = (bf16[512,128]{1,0:T(8,128)(2,1)S(1)}, bf16[512,128]{1,0:T(8,128)(2,1)}, u32[]{:S(2)}) copy-start(bf16[512,128]{1,0:T(8,128)(2,1)} %param.6) | copy-start | bytes 393220
where the time goes:
time: 70.3 us; the launch traced here: 70 us
  blocking collectives  21.4 us (30%)
  matrix products  16.2 us (23%)
  waiting for transfers between devices  12.6 us (18%)
  starting transfers between devices  9.39 us (13%)
  other arithmetic  7.36 us (10%)
  local copies, waits for them, and re-layouts  2.83 us (4%)
    all_to_all x1, blocking collectives, per_device(): lax.all_to_all(merged, 'head', split_axis=0, concat_axis=1, tiled=True)  21.4 us
    ppermute x4, waiting for transfers between devices, from_behind(): return lax.ppermute(x, axis, pairs)  12.6 us
    ppermute x4, starting transfers between devices, from_behind(): return lax.ppermute(x, axis, pairs)  9.39 us
    dot_general x4, matrix products, per_device(): jnp.dot(weights.astype(jnp.bfloat16), value_window, preferred_element_typ...  8.8 us
    dot_general x4, matrix products, per_device(): lax.dot_general(query_head, key_window, (((1,), (1,)), ((), ())), preferr...  7.4 us
    reduce_sum x1, other arithmetic, per_device(): total = jnp.sum(weights, axis=1, keepdims=True)  4.95 us
  transfers between devices with their start and end apart: 4, of which 2 were waited for; matrix products, arithmetic and copies ran while one was open for 9% of the time, Pallas kernels for 0%

commit v1 on v0

v1 whole, which is shorter than its diff:
```python
import jax
import jax.numpy as jnp
from jax import lax
from jax.experimental import pallas as pl
from jax.experimental.pallas import tpu as pltpu
from jax.sharding import PartitionSpec as P

HD = 128
GROUP = 4
T = 512
LANES = 128
FAR = 4194304.0
SCALE = 0.08838834764831845 * 1.4426950408889634
QT = 256


def attention_kernel(where_ref, docs_ref, q_ref, k_ref, v_ref, x_ref, a_ref, s_ref, o_ref, kw, vw):
    first, odd = where_ref[0], where_ref[1]
    begins, ends = docs_ref[0:1, :], docs_ref[1:2, :]
    ones = jnp.ones((T, HD), jnp.bfloat16)

    def inside(base, rows):
        position = base + lax.broadcasted_iota(jnp.int32, (rows, LANES), 0)
        return (position >= begins) & (position < ends)

    def put(slot, keys, values):
        rows = pl.ds(pl.multiple_of(slot * T, T), T)
        kw[rows, :HD] = keys
        kw[rows, HD:] = jnp.where(inside(first + (slot - 3) * T, T), 0.0, -FAR).astype(jnp.bfloat16)
        vw[rows, :HD] = values
        vw[rows, HD:] = ones

    put(3, k_ref[...], v_ref[...])
    put(1, a_ref[:, :HD], a_ref[:, HD:])
    put(2 * odd, x_ref[:, :HD], x_ref[:, HD:])
    put(2 - 2 * odd, s_ref[:, :HD], s_ref[:, HD:])
    causal = lax.broadcasted_iota(jnp.int32, (QT, QT), 1) <= lax.broadcasted_iota(jnp.int32, (QT, QT), 0)
    for low in range(0, T, QT):
        window = slice(low, low + 3 * T + QT)
        own = jnp.where(inside(first + low, QT), 1.0, 0.0).astype(jnp.bfloat16)
        for head in range(GROUP):
            columns = slice(head * HD, (head + 1) * HD)
            query = jnp.concatenate([q_ref[low : low + QT, columns], own], 1)
            scores = lax.dot_general(
                query, kw[window, :], (((1,), (1,)), ((), ())), preferred_element_type=jnp.float32
            )
            scores = jnp.concatenate(
                [scores[:, : 3 * T], jnp.where(causal, scores[:, 3 * T :], -FAR)], 1
            )
            largest = jnp.max(scores, axis=1, keepdims=True)
            weights = jnp.exp2((scores - largest) * SCALE).astype(jnp.bfloat16)
            mixed = jnp.dot(weights, vw[window, :], preferred_element_type=jnp.float32)
            o_ref[low : low + QT, columns] = (mixed[:, :HD] / mixed[:, HD:]).astype(jnp.bfloat16)


def attention(where, docs, queries, keys, values, x, a, s):
    vmem = pl.BlockSpec(memory_space=pltpu.VMEM)
    return pl.pallas_call(
        attention_kernel,
        out_shape=jax.ShapeDtypeStruct((T, GROUP * HD), jnp.bfloat16),
        in_specs=[pl.BlockSpec(memory_space=pltpu.SMEM)] + [vmem] * 7,
        out_specs=vmem,
        scratch_shapes=[pltpu.VMEM((4 * T, 2 * HD), jnp.bfloat16)] * 2,
        compiler_params=pltpu.CompilerParams(vmem_limit_bytes=32 << 20),
        cost_estimate=pl.CostEstimate(flops=4 * 10**9, transcendentals=4 * 10**6, bytes_accessed=3 * 10**6),
        name="attention",
    )(where, docs, queries, keys, values, x, a, s)


def per_device(queries, key_rows, value_rows, doc_lengths):
    blocks = lax.axis_size("seq")
    block = lax.axis_index("seq")
    rows = jnp.concatenate([key_rows, value_rows], 1)
    a = lax.ppermute(rows, "seq", [(i, i + 2) for i in range(blocks - 2)])
    hops = [(i, i + 1 if i % 2 == 0 else i + 3) for i in range(blocks)]
    x = lax.ppermute(rows, "seq", [(i, j) for i, j in hops if j < blocks])
    s = lax.ppermute(a, "seq", [(i, i ^ 1) for i in range(blocks)])
    lengths = jnp.pad(doc_lengths, (0, LANES - doc_lengths.shape[0]))
    index = jnp.arange(LANES, dtype=jnp.int32)
    ends = jnp.sum(jnp.where(index[:, None] >= index[None, :], lengths[None, :], 0), axis=1)
    docs = jnp.stack([ends - lengths, ends])
    where = jnp.stack([block * T, block % 2]).astype(jnp.int32)
    merged = attention(where, docs, queries, key_rows, value_rows, x, a, s)
    return lax.all_to_all(merged, "head", split_axis=0, concat_axis=1, tiled=True)


def solution(mesh):
    in_specs = (P("seq", "head"), P("seq", "head"), P("seq", "head"), P())
    out_specs = P(("seq", "head"), None)
    return jax.shard_map(
        per_device, mesh=mesh, in_specs=in_specs, out_specs=out_specs, check_vma=False
    )
```

time: 70.3 us -> 52.4 us (0.75)
  matrix products: 16.2 us -> 0 us
  other arithmetic: 7.36 us -> 0.19 us
  Pallas kernels: 0 us -> 5.93 us
  blocking collectives: 21.4 us -> 24.7 us
  starting transfers between devices: 9.39 us -> 7.36 us
  waiting for transfers between devices: 12.6 us -> 10.9 us
    dot_general x8 -> x0, matrix products: 16.2 us -> none  [the longest x4 8.8 us: per_device(): jnp.dot(weights.astype(jnp.bfloat16), value_window, preferred_element_typ...]
    pallas_call x0 -> x1, Pallas kernels: none -> 5.93 us  [attention(): pl.pallas_call(attention_kernel, out_shape=jax.ShapeDtypeStruct((T, GROUP...]
    reduce_sum x3 -> x1, other arithmetic: 5.22 us -> 0.1 us  [per_device(): jnp.sum(jnp.where(index[:, None] >= index[None, :], lengths[None, :], 0),...]
    all_to_all x1, blocking collectives: 21.4 us -> 24.7 us  [per_device(): lax.all_to_all(merged, 'head', split_axis=0, concat_axis=1, tiled=True)]
    ppermute x4 -> x3, starting transfers between devices: 9.39 us -> 7.36 us  [the longest x1 3.53 us: per_device(): a = lax.ppermute(rows, 'seq', [(i, i + 2) for i in range(blocks - 2)])]
    unnamed x8 -> x9, local copies, waits for them, and re-layouts: 0.09 us -> 2.02 us
    concatenate x3 -> x0, other arithmetic: 1.88 us -> none  [the longest x1 0.92 us: per_device(): value_window = jnp.concatenate([moved[1], value_window], 0)]
    ppermute x4 -> x3, waiting for transfers between devices: 12.6 us -> 10.9 us  [the longest x1 9.53 us: per_device(): a = lax.ppermute(rows, 'seq', [(i, i + 2) for i in range(blocks - 2)])]
  transfers between devices with their start and end apart: 4 -> 3, of which waited for: 2 -> 2; matrix products, arithmetic and copies ran while one was open for 9% -> 0% of each run, Pallas kernels for 0% -> 0%
where the time goes in v1:
time: 52.4 us; the launch traced here: 52.1 us
  blocking collectives  24.7 us (47%)
  waiting for transfers between devices  10.9 us (21%)
  starting transfers between devices  7.36 us (14%)
  Pallas kernels  5.93 us (11%)
  local copies, waits for them, and re-layouts  2.89 us (6%)
    all_to_all x1, blocking collectives, per_device(): lax.all_to_all(merged, 'head', split_axis=0, concat_axis=1, tiled=True)  24.7 us
    ppermute x1, waiting for transfers between devices, per_device(): a = lax.ppermute(rows, 'seq', [(i, i + 2) for i in range(blocks - 2)])  9.53 us
    pallas_call x1, Pallas kernels, attention(): pl.pallas_call(attention_kernel, out_shape=jax.ShapeDtypeStruct((T, GROUP...  5.93 us
    ppermute x1, starting transfers between devices, per_device(): a = lax.ppermute(rows, 'seq', [(i, i + 2) for i in range(blocks - 2)])  3.53 us
    unnamed x9, local copies, waits for them, and re-layouts  2.02 us
    ppermute x1, starting transfers between devices, per_device(): x = lax.ppermute(rows, 'seq', [(i, j) for i, j in hops if j < blocks])  1.92 us
    ppermute x1, starting transfers between devices, per_device(): s = lax.ppermute(a, 'seq', [(i, i ^ 1) for i in range(blocks)])  1.91 us
    ppermute x1, waiting for transfers between devices, per_device(): s = lax.ppermute(a, 'seq', [(i, i ^ 1) for i in range(blocks)])  1.38 us
  transfers between devices with their start and end apart: 3, of which 2 were waited for; matrix products, arithmetic and copies ran while one was open for 0% of the time, Pallas kernels for 0%

profile of v1, /device:TPU:512, one launch (start us, length us, event | category | flops | bytes accessed | tf_op | source)
XLA Modules:
  0.0 52.1 jit_solution(15438055482547227091)
XLA Ops:
  0.0 0.0 copy-start.1
  0.0 1.0 %constant_dynamic-update-slice_fusion.1 = bf16[512,256]{1,0:T(8,128)(2,1)S(1)} fusion(bf16[512,128]{1,0:T(8,128)(2,1)} %k_ref.1), kind=kLoop, calls=%fused_computation.3 | loop fusion | bytes 262144
  1.0 0.0 copy-done.1
  1.0 0.0 copy-start.3
  1.0 0.0 copy-start
  1.0 3.5 %collective-permute-start.1 = (bf16[512,256]{1,0:T(8,128)(2,1)S(1)}, bf16[512,256]{1,0:T(8,128)(2,1)S(1)}, u32[]{:S(2)}, u32[]{:S(2)}) collective-permute-start(bf16[512,256]{1,0:T(8,128)(2,1)S(1)} %constant_dynamic-update-slice_fusion), channel_id=1, source_target_pairs={{0,16},{8,24},{16,32},{24,40},{32,48},{40,56},{48,64},{56,72},{64,... | collective-permute-start | bytes 786440 | tf_op jit(solution)/shard_map/ppermute | solution.py:74
  4.6 1.9 %collective-permute-start = (bf16[512,256]{1,0:T(8,128)(2,1)S(1)}, bf16[512,256]{1,0:T(8,128)(2,1)S(1)}, u32[]{:S(2)}, u32[]{:S(2)}) collective-permute-start(bf16[512,256]{1,0:T(8,128)(2,1)S(1)} %constant_dynamic-update-slice_fusion), channel_id=1, source_target_pairs={{0,8},{8,32},{16,24},{24,48},{32,40},{40,64},{48,56},{56,80},{64,7... | collective-permute-start | bytes 786440 | tf_op jit(solution)/shard_map/ppermute | solution.py:76
  6.5 0.0 copy-done.3
  6.5 0.1 select_reduce_fusion
  6.6 9.5 %collective-permute-done.1.a_ref = bf16[512,256]{1,0:T(8,128)(2,1)S(1)} collective-permute-done((bf16[512,256]{1,0:T(8,128)(2,1)S(1)}, bf16[512,256]{1,0:T(8,128)(2,1)S(1)}, u32[]{:S(2)}, u32[]{:S(2)}) %collective-permute-start.1) | collective-permute-done | bytes 262176 | tf_op jit(solution)/shard_map/ppermute | solution.py:74
  16.2 1.9 %collective-permute-start.2 = (bf16[512,256]{1,0:T(8,128)(2,1)S(1)}, bf16[512,256]{1,0:T(8,128)(2,1)S(1)}, u32[]{:S(2)}, u32[]{:S(2)}) collective-permute-start(bf16[512,256]{1,0:T(8,128)(2,1)S(1)} %collective-permute-done.1.a_ref), channel_id=1, source_target_pairs={{0,8},{8,0},{16,24},{24,16},{32,40},{40,32},{48,56},{56,48},{64,72... | collective-permute-start | bytes 786440 | tf_op jit(solution)/shard_map/ppermute | solution.py:77
  18.1 0.1 pad_add_fusion.1.where_ref
  18.2 0.0 collective-permute-done.x_ref
  18.2 1.4 %collective-permute-done.2.s_ref = bf16[512,256]{1,0:T(8,128)(2,1)S(1)} collective-permute-done((bf16[512,256]{1,0:T(8,128)(2,1)S(1)}, bf16[512,256]{1,0:T(8,128)(2,1)S(1)}, u32[]{:S(2)}, u32[]{:S(2)}) %collective-permute-start.2) | collective-permute-done | bytes 262176 | tf_op jit(solution)/shard_map/ppermute | solution.py:77
  19.6 0.0 copy-done
  19.6 0.0 copy-start.2
  19.6 1.0 %copy-done.2 = bf16[512,512]{1,0:T(8,128)(2,1)S(1)} copy-done((bf16[512,512]{1,0:T(8,128)(2,1)S(1)}, bf16[512,512]{1,0:T(8,128)(2,1)}, u32[]{:S(2)}) %copy-start.2) | copy-done | bytes 524312
  20.6 5.9 %attention.1 = bf16[512,512]{1,0:T(8,128)(2,1)S(1)} custom-call(s32[2]{0:T(128)S(1)} %pad_add_fusion.1.where_ref, s32[2,128]{1,0:T(2,128)S(1)} %pad_add_fusion.docs_ref, bf16[512,512]{1,0:T(8,128)(2,1)S(1)} %copy-done.2, bf16[512,128]{1,0:T(8,128)(2,1)S(1)} %copy-done, bf16[512,128]{1,0:T(8,128)(2,1)S(1)} %copy-done.1, ...), custom_call_target="tpu_custom_call" | custom-call | flops 4000000000 | bytes 3000000 | tf_op jit(solution)/shard_map/attention/pallas_call | solution.py:58
  26.6 24.7 %all_to_all.19 = bf16[8,64,512]{2,1,0:T(8,128)(2,1)S(1)} all-to-all(bf16[8,64,512]{2,1,0:T(8,128)(2,1)S(1)} %bitcast.9), channel_id=1, replica_groups=mesh['seq'=96,'head'=8] {'head'}, dimensions={0} | all-to-all | bytes 1048576 | tf_op jit(solution)/shard_map/all_to_all | solution.py:84
  51.3 0.8 %copy.7 = bf16[8,8,8,512]{3,2,0,1:T(8,128)(2,1)} copy(bf16[8,8,8,512]{3,2,1,0:T(8,128)(2,1)S(1)} %bitcast.10) | data formatting | bytes 1048576 | tf_op jit(solution)/shard_map/all_to_all | solution.py:84
  (4 shorter events, 0.1 us)
Async XLA Ops:
  0.0 1.0 %copy-start.1 = (bf16[512,128]{1,0:T(8,128)(2,1)S(1)}, bf16[512,128]{1,0:T(8,128)(2,1)}, u32[]{:S(2)}) copy-start(bf16[512,128]{1,0:T(8,128)(2,1)} %v_ref.1) | copy-start | bytes 393220
  1.0 5.5 %copy-start.3 = (s32[96]{0:T(128)S(1)}, s32[96]{0:T(128)}, u32[]{:S(2)}) copy-start(s32[96]{0:T(128)} %param.7) | copy-start | bytes 1156
  1.0 18.6 %copy-start = (bf16[512,128]{1,0:T(8,128)(2,1)S(1)}, bf16[512,128]{1,0:T(8,128)(2,1)}, u32[]{:S(2)}) copy-start(bf16[512,128]{1,0:T(8,128)(2,1)} %k_ref.1) | copy-start | bytes 393220
  1.0 15.1 %collective-permute-start.1 = (bf16[512,256]{1,0:T(8,128)(2,1)S(1)}, bf16[512,256]{1,0:T(8,128)(2,1)S(1)}, u32[]{:S(2)}, u32[]{:S(2)}) collective-permute-start(bf16[512,256]{1,0:T(8,128)(2,1)S(1)} %constant_dynamic-update-slice_fusion), channel_id=1, source_target_pairs={{0,16},{8,24},{16,32},{24,40},{32,48},{40,56},{48,64},{56,72},{64,... | collective-permute-start | bytes 786440 | tf_op jit(solution)/shard_map/ppermute | solution.py:74
  4.6 13.6 %collective-permute-start = (bf16[512,256]{1,0:T(8,128)(2,1)S(1)}, bf16[512,256]{1,0:T(8,128)(2,1)S(1)}, u32[]{:S(2)}, u32[]{:S(2)}) collective-permute-start(bf16[512,256]{1,0:T(8,128)(2,1)S(1)} %constant_dynamic-update-slice_fusion), channel_id=1, source_target_pairs={{0,8},{8,32},{16,24},{24,48},{32,40},{40,64},{48,56},{56,80},{64,7... | collective-permute-start | bytes 786440 | tf_op jit(solution)/shard_map/ppermute | solution.py:76
  16.2 3.4 %collective-permute-start.2 = (bf16[512,256]{1,0:T(8,128)(2,1)S(1)}, bf16[512,256]{1,0:T(8,128)(2,1)S(1)}, u32[]{:S(2)}, u32[]{:S(2)}) collective-permute-start(bf16[512,256]{1,0:T(8,128)(2,1)S(1)} %collective-permute-done.1.a_ref), channel_id=1, source_target_pairs={{0,8},{8,0},{16,24},{24,16},{32,40},{40,32},{48,56},{56,48},{64,72... | collective-permute-start | bytes 786440 | tf_op jit(solution)/shard_map/ppermute | solution.py:77
  19.6 1.0 %copy-start.2 = (bf16[512,512]{1,0:T(8,128)(2,1)S(1)}, bf16[512,512]{1,0:T(8,128)(2,1)}, u32[]{:S(2)}) copy-start(bf16[512,512]{1,0:T(8,128)(2,1)} %q_ref.1) | copy-start | bytes 1572868
